TPU v7x, 32 devices: a whole 2x2x4 slice. The times are simulated.
32 devices in a mesh: seq: 16 (over z, y, core), exp: 2 (over x).
Axes of the slice: x: 2, y: 2, z: 4, core: 2. Of those that a mesh axis runs over, the one named last changes fastest.
Arguments:
- hidden_in: bfloat16 [6, 6144], P('exp', 'seq'), may hold values from -2 to 2
- queries: bfloat16 [6, 6144], P(None, 'exp'), may hold values from -40 to 40
- key_cache: bfloat16 [6, 8192, 1024], P(None, 'seq', 'exp'), may hold values from -16 to 16
- value_cache: bfloat16 [6, 8192, 1024], P(None, 'seq', 'exp'), may hold values from -6 to 6
- lengths: int32 [6], replicated, may hold values from 2 to 8192
- out_weight: bfloat16 [6144, 6144], P('exp', 'seq'), may hold values from -0.078125 to 0.078125
- norm_gain: float32 [6144], P('seq'), may hold values from 0.1 to 1.9
- router: bfloat16 [6144, 8], P('seq'), may hold values from -0.078125 to 0.078125
- expert_ids: int32 [6, 2], P('exp'), may hold values from 0 to 7, as said below
- capacity: int32 [8], replicated, may hold values from 1 to 3, as said below
- w_gate: bfloat16 [8, 6144, 8192], P('exp', None, 'seq'), may hold values from -0.078125 to 0.078125
- w_up: bfloat16 [8, 6144, 8192], P('exp', None, 'seq'), may hold values from -0.078125 to 0.078125
- w_down: bfloat16 [8, 8192, 6144], P('exp', 'seq'), may hold values from -0.09375 to 0.09375
Outputs:
- layer_out: bfloat16 [6, 6144], P('exp', 'seq')
Inputs may be any that keep to these rules, and one draw needn't show every extreme that they name: lengths[b] counts sequence b's live cache positions, the newest token's included. `expert_ids`: the two experts of a token differ. One expert is named by every token; any other expert is named at most 3 times within one aligned block of 3 tokens. The expert that every token names has capacity 3.
All inputs are finite; a program needn't handle non-finite values.
Results may differ from a plain program's by a relative error of at most 0.0085.
Values may be sent and summed in bfloat16 or wider, within the bound.
A program may use at most 128 MiB of HBM per device.

v0:
```python
import math

import jax
import jax.numpy as jnp
from jax import lax
from jax.sharding import PartitionSpec as P

D = 6144
HEADS = 48
KV_HEADS = 8
HEAD_DIM = 128
EXPERTS = 8


masked_score = -1e30
norm_eps = 1e-05


def joined(value, axis, join):
    pieces = jax.tree.map(lambda part: lax.all_gather(part, axis), value)
    head = jax.tree.map(lambda part: part[0], pieces)
    tail = jax.tree.map(lambda part: part[1:], pieces)
    running, _ = lax.scan(lambda running, share: (join(running, share), None), head, tail)
    return running


def merge_partial_results(left_part, right_part):
    left_maximum_score, left_denom, left_sum = left_part
    right_peak, right_denom, right_sum = right_part
    joint_peak = jnp.maximum(left_maximum_score, right_peak)
    left_factor = jnp.exp(left_maximum_score - joint_peak)
    right_factor = jnp.exp(right_peak - joint_peak)
    return (
        joint_peak,
        left_denom * left_factor + right_denom * right_factor,
        left_sum * left_factor[..., None] + right_sum * right_factor[..., None],
    )


def on_device(
    hidden_in,
    queries,
    key_cache,
    value_cache,
    lengths,
    out_weight,
    norm_gain,
    router,
    expert_ids,
    capacity,
    w_gate,
    w_up,
    w_down,
):
    seq_count = queries.shape[0]
    group_size = HEADS // KV_HEADS
    kv_local = key_cache.shape[2] // HEAD_DIM
    span_local = key_cache.shape[1]
    query_heads = queries.reshape(seq_count, kv_local, group_size, HEAD_DIM)
    key_rows = key_cache.reshape(seq_count, span_local, kv_local, HEAD_DIM)
    value_rows = value_cache.reshape(seq_count, span_local, kv_local, HEAD_DIM).astype(jnp.float32)
    first_place = lax.axis_index("seq") * span_local
    places = first_place + jnp.arange(span_local, dtype=jnp.int32)
    live_mask = (places[None, :] < lengths[:, None])[:, None, None, :]
    scores = jnp.einsum(
        "bkgd,bjkd->bkgj", query_heads, key_rows, preferred_element_type=jnp.float32
    ) * (1.0 / math.sqrt(HEAD_DIM))
    scores = jnp.where(live_mask, scores, masked_score)
    local_peak = jnp.max(scores, axis=-1)
    attn_weights = jnp.where(live_mask, jnp.exp(scores - local_peak[..., None]), 0.0)
    local_sum = jnp.einsum(
        "bkgj,bjkd->bkgd", attn_weights, value_rows, precision=lax.Precision.HIGHEST
    )
    global_peak, denom_sum, weighted = joined(
        (local_peak, jnp.sum(attn_weights, axis=-1), local_sum), "seq", merge_partial_results
    )
    attended = (
        (weighted / denom_sum[..., None])
        .reshape(seq_count, kv_local * group_size * HEAD_DIM)
        .astype(jnp.bfloat16)
    )
    partial_value = jnp.dot(attended, out_weight, preferred_element_type=jnp.float32)
    projected = lax.psum_scatter(partial_value, "exp", scatter_dimension=0, tiled=True)
    residual = hidden_in.astype(jnp.float32) + projected
    gained = residual * norm_gain
    router_wide = router.astype(jnp.float32)
    squares = jnp.sum(residual * residual, axis=-1)
    total_sq = lax.psum(squares, "seq")
    scale_row = lax.rsqrt(total_sq / D + norm_eps)
    logits = lax.psum(
        jnp.dot(gained * scale_row[:, None], router_wide, precision=lax.Precision.HIGHEST), "seq"
    )
    normed = (gained * scale_row[:, None]).astype(jnp.bfloat16)
    row_total = expert_ids.shape[0]
    onehot_int = (
        expert_ids[:, :, None] == jnp.arange(EXPERTS, dtype=jnp.int32)[None, None, :]
    ).astype(jnp.int32)
    name_count = jnp.sum(onehot_int, axis=1)
    row_order = jnp.arange(row_total, dtype=jnp.int32)
    before = (row_order[None, :] < row_order[:, None]).astype(jnp.int32)
    earlier = jnp.dot(before, name_count)
    slot_rank = jnp.sum(onehot_int * earlier[:, None, :], axis=-1)
    slot_limit = jnp.sum(onehot_int * capacity[None, None, :], axis=-1)
    kept_mask = (slot_rank < slot_limit).astype(jnp.float32)
    expert_indicator = onehot_int.astype(jnp.float32)
    chosen = jnp.sum(expert_indicator * logits[:, None, :], axis=-1)
    gate_weight = jax.nn.sigmoid(chosen - chosen[:, ::-1])
    slot_match = (slot_rank[:, :, None] == row_order[None, None, :]).astype(jnp.float32)
    placing = jnp.einsum("rke,rks->esr", expert_indicator * kept_mask[:, :, None], slot_match)
    buffer = jnp.einsum(
        "esr,rd->esd", placing.astype(jnp.bfloat16), normed, preferred_element_type=jnp.float32
    ).astype(jnp.bfloat16)
    dispatched = lax.all_to_all(buffer, "exp", split_axis=0, concat_axis=1, tiled=True)
    shard_rows = lax.all_gather(dispatched, "seq", axis=2, tiled=True)
    gate_next = jnp.einsum("ern,enf->erf", shard_rows, w_gate, preferred_element_type=jnp.float32)
    up_next = jnp.einsum("ern,enf->erf", shard_rows, w_up, preferred_element_type=jnp.float32)
    hidden_act = (jax.nn.silu(gate_next) * up_next).astype(jnp.bfloat16)
    partial_out = jnp.einsum("erf,efd->erd", hidden_act, w_down, preferred_element_type=jnp.float32)
    blend_table = jnp.einsum(
        "rke,rks->esr", expert_indicator * (gate_weight * kept_mask)[:, :, None], slot_match
    )
    reduced_output = lax.psum_scatter(partial_out, "seq", scatter_dimension=2, tiled=True)
    returned = lax.all_to_all(reduced_output, "exp", split_axis=1, concat_axis=0, tiled=True)
    combined = jnp.einsum("esr,esd->rd", blend_table, returned, precision=lax.Precision.HIGHEST)
    return (residual + combined).astype(jnp.bfloat16)


def solution(mesh):
    in_specs = (
        P("exp", "seq"),
        P(None, "exp"),
        P(None, "seq", "exp"),
        P(None, "seq", "exp"),
        P(),
        P("exp", "seq"),
        P("seq"),
        P("seq", None),
        P("exp", None),
        P(),
        P("exp", None, "seq"),
        P("exp", None, "seq"),
        P("exp", "seq", None),
    )
    out_specs = P("exp", "seq")
    return jax.shard_map(
        on_device, mesh=mesh, in_specs=in_specs, out_specs=out_specs, check_vma=False
    )
```

profile of v0, /device:TPU:0, one launch (start us, length us, event | category | flops | bytes accessed | tf_op | source)
XLA Modules:
  0.0 272.3 jit_solution(8240845647066863271)
XLA Ops:
  6.5 1.6 reshape.56
  8.2 0.9 broadcast_compare_fusion
  9.1 1.8 fusion.49
  10.9 1.4 fusion.4
  12.3 0.7 copy.28
  13.1 23.7 %all-gather = f32[96,4,6]{2,1,0:T(4,128)S(1)} all-gather(f32[6,4,6]{2,1,0:T(4,128)S(1)} %get-tuple-element.74), channel_id=2, replica_groups=mesh['seq'=16,'exp'=2] {'seq'}, dimensions={0}, use_global_device_ids=true | all-gather | bytes 9792 | tf_op jit(solution)/shard_map/all_gather | solution.py:20
  36.8 0.2 fusion.20
  37.0 18.4 %all-gather.1 = f32[96,4,6]{2,1,0:T(4,128)S(1)} all-gather(f32[6,4,6]{2,1,0:T(4,128)S(1)} %fusion.20), channel_id=3, replica_groups=mesh['seq'=16,'exp'=2] {'seq'}, dimensions={0}, use_global_device_ids=true | all-gather | bytes 9792 | tf_op jit(solution)/shard_map/all_gather | solution.py:20
  55.5 0.7 dynamic-slice
  57.0 0.9 slice.32
  57.9 2.3 slice.35
  60.3 16.4 %while.14 = (s32[]{:T(128)}, f32[6,4,6]{2,1,0:T(4,128)S(1)}, f32[6,4,6]{2,1,0:T(4,128)S(1)}, f32[6,4,6,128]{3,2,1,0:T(8,128)S(1)}, f32[15,6,4,6]{3,2,1,0:T(4,128...) while((s32[]{:T(128)}, f32[6,4,6]{2,1,0:T(4,128)S(1)}, ...), condition=%wide.region_3.4_spmd, body=%wide.region_2.3_spmd.sunk | while | flops 56162 | bytes 374501 | solution.py:23
  60.3 0.9 constant_dynamic-slice_fusion.2
  61.2 0.1 fusion.70
  61.4 0.9 constant_dynamic-slice_fusion.2
  62.5 0.9 constant_dynamic-slice_fusion.2
  63.6 0.9 constant_dynamic-slice_fusion.2
  64.7 0.9 constant_dynamic-slice_fusion.2
  65.8 0.9 constant_dynamic-slice_fusion.2
  66.9 0.9 constant_dynamic-slice_fusion.2
  67.9 0.9 constant_dynamic-slice_fusion.2
  69.0 0.9 constant_dynamic-slice_fusion.2
  70.1 0.9 constant_dynamic-slice_fusion.2
  71.2 0.9 constant_dynamic-slice_fusion.2
  72.3 0.9 constant_dynamic-slice_fusion.2
  73.4 0.9 constant_dynamic-slice_fusion.2
  74.5 0.9 constant_dynamic-slice_fusion.2
  75.6 0.9 constant_dynamic-slice_fusion.2
  76.8 0.4 fusion.50
  77.2 8.1 %all-reduce = f32[6,384]{1,0:T(8,128)S(1)} all-reduce(f32[6,384]{1,0:T(8,128)S(1)} %fusion.50), channel_id=5, replica_groups=mesh['seq'=16,'exp'=2] {'exp'}, use_global_device_ids=true, to_apply=%region_4.5.clone | all-reduce | flops 2304 | bytes 18432
  85.5 29.5 %psum.14 = f32[3]{0:T(128)S(1)} all-reduce(f32[3]{0:T(128)S(1)} %multiply_reduce_fusion), channel_id=1, replica_groups=mesh['seq'=16,'exp'=2] {'seq'}, use_global_device_ids=true, to_apply=%region_9.10 | all-reduce | flops 3 | bytes 24 | tf_op jit(solution)/shard_map/psum | solution.py:88
  115.0 0.2 fusion.26
  115.2 0.3 select_reduce_fusion
  115.5 29.5 %psum.15 = f32[3,8]{1,0:T(4,128)S(1)} all-reduce(f32[3,8]{1,0:T(4,128)S(1)} %fusion.26), channel_id=1, replica_groups=mesh['seq'=16,'exp'=2] {'seq'}, use_global_device_ids=true, to_apply=%region_10.11 | all-reduce | flops 24 | bytes 192 | tf_op jit(solution)/shard_map/psum | solution.py:90
  145.0 0.2 fusion.30
  145.2 0.3 fusion.19
  145.5 0.2 convolution_convert_fusion
  145.7 6.3 %all_to_all.36 = bf16[8,3,384]{2,1,0:T(4,128)(2,1)S(1)} all-to-all(bf16[8,3,384]{2,1,0:T(4,128)(2,1)S(1)} %copy.33), channel_id=1, replica_groups=mesh['seq'=16,'exp'=2] {'exp'}, dimensions={0} | all-to-all | bytes 36864 | tf_op jit(solution)/shard_map/all_to_all | solution.py:113
  152.0 18.3 %all_gather.27 = bf16[4,6,6144]{2,1,0:T(8,128)(2,1)S(1)} all-gather(bf16[4,6,384]{2,1,0:T(8,128)(2,1)S(1)} %copy.35), channel_id=1, replica_groups=mesh['seq'=16,'exp'=2] {'seq'}, dimensions={2}, use_global_device_ids=true | all-gather | bytes 313344 | tf_op jit(solution)/shard_map/all_gather | solution.py:114
  170.3 9.9 %fusion.51 = f32[4,6,512]{2,1,0:T(8,128)S(1)} fusion(bf16[4,6,6144]{2,1,0:T(8,128)(2,1)S(1)} %all_gather.27, bf16[4,6144,512]{2,1,0:T(8,128)(2,1)} %param.25), kind=kOutput, calls=%fused_computation.70 | convolution fusion | flops 150994944 | bytes 25509888 | tf_op jit(solution)/shard_map/ern,enf->erf/dot_general | solution.py:115
  180.2 9.9 %fusion.16 = bf16[4,6,512]{2,1,0:T(8,128)(2,1)S(1)} fusion(bf16[4,6,6144]{2,1,0:T(8,128)(2,1)S(1)} %all_gather.27, bf16[4,6144,512]{2,1,0:T(8,128)(2,1)} %param.26, f32[4,6,512]{2,1,0:T(8,128)S(1)} %fusion.51), kind=kOutput, calls=%fused_computation.19 | convolution fusion | flops 151068672 | bytes 25534464 | tf_op jit(solution)/shard_map/ern,enf->erf/dot_general | solution.py:116
  190.1 10.9 %fusion.52 = f32[4,6,6144]{2,1,0:T(8,128)} fusion(bf16[4,6,512]{2,1,0:T(8,128)(2,1)S(1)} %fusion.16, bf16[4,512,6144]{2,1,0:T(8,128)(2,1)} %param.27), kind=kOutput, calls=%fused_computation.71 | convolution fusion | flops 150994944 | bytes 25780224 | tf_op jit(solution)/shard_map/erf,efd->erd/dot_general | solution.py:118
  201.1 54.9 %reduce-scatter.2.cloned.1.call-done = f32[4,6,384]{2,1,0:T(8,128)} async-done(((f32[4,6,6144]{2,1,0:T(8,128)}), f32[4,6,384]{2,1,0:T(8,128)}) %reduce-scatter.2.cloned.1.call-update) | async-done | bytes 36880 | tf_op jit(solution)/shard_map/reduce_scatter | solution.py:122
  255.9 1.4 copy.36
  257.4 3.3 %all-to-all-start.1 = ((f32[4,6,384]{2,0,1:T(4,128)}), f32[4,6,384]{2,0,1:T(4,128)S(1)}, u32[]{:S(2)}, u32[]{:S(2)}) async-start(f32[4,6,384]{2,0,1:T(4,128)} %copy.36), calls=%async_computation.2 | async-start | bytes 73728 | tf_op jit(solution)/shard_map/all_to_all | solution.py:123
  260.6 0.3 convolution_bitcast_fusion.1
  260.9 3.7 %all-to-all-done.1 = f32[4,6,384]{2,0,1:T(4,128)S(1)} async-done(((f32[4,6,384]{2,0,1:T(4,128)}), f32[4,6,384]{2,0,1:T(4,128)S(1)}, u32[]{:S(2)}, u32[]{:S(2)}) %all-to-all-start.1) | async-done | bytes 36896 | tf_op jit(solution)/shard_map/all_to_all | solution.py:123
  264.6 0.8 fusion.18
  (75 shorter events, 3.4 us)
Async XLA Ops:
  6.5 2.5 copy-start
  6.5 50.4 %all-gather.5.cloned.1.call-start = ((), (), s32[]{:S(2)}) async-start(), calls=%async_computation.4 | async-start | bytes 1253376 | tf_op jit(solution)/shard_map/all_gather | solution.py:20
  8.2 2.7 %copy-start.2 = (bf16[6,512,512]{2,1,0:T(8,128)(2,1)S(1)}, bf16[6,512,512]{2,1,0:T(8,128)(2,1)}, u32[]{:S(2)}) copy-start(bf16[6,512,512]{2,1,0:T(8,128)(2,1)} %param.18) | copy-start | bytes 9437188
  10.9 44.5 %copy-start.5 = (s32[3,2]{0,1:T(2,128)S(1)}, s32[3,2]{0,1:T(2,128)}, u32[]{:S(2)}) copy-start(s32[3,2]{0,1:T(2,128)} %param.23) | copy-start | bytes 76
  10.9 44.6 %copy-start.9 = (u32[32]{0:T(128)S(1)}, u32[32]{0:T(128)}, u32[]{:S(2)}) copy-start(u32[32]{0:T(128)} %constant.44) | copy-start | bytes 388
  13.0 242.9 %reduce-scatter.2.cloned.1.call-start = ((), (), s32[]{:S(2)}) async-start(), calls=%async_computation.3 | async-start | bytes 835584 | tf_op jit(solution)/shard_map/reduce_scatter | solution.py:122
  37.0 39.8 %copy-start.3 = (bf16[3072,384]{1,0:T(8,128)(2,1)S(1)}, bf16[3072,384]{1,0:T(8,128)(2,1)}, u32[]{:S(2)}) copy-start(bf16[3072,384]{1,0:T(8,128)(2,1)} %param.20) | copy-start | bytes 7077892
  60.2 25.0 %copy-start.4 = (bf16[3,384]{1,0:T(4,128)(2,1)S(1)}, bf16[3,384]{1,0:T(4,128)(2,1)}, u32[]{:S(2)}) copy-start(bf16[3,384]{1,0:T(4,128)(2,1)} %param.15) | copy-start | bytes 6916
  60.3 54.8 %copy-start.7 = (bf16[384,8]{0,1:T(8,128)(2,1)S(1)}, bf16[384,8]{0,1:T(8,128)(2,1)}, u32[]{:S(2)}) copy-start(bf16[384,8]{0,1:T(8,128)(2,1)} %param.22) | copy-start | bytes 18436
  60.3 54.8 %copy-start.8 = (f32[384]{0:T(512)S(1)}, f32[384]{0:T(512)}, u32[]{:S(2)}) copy-start(f32[384]{0:T(512)} %param.21) | copy-start | bytes 4612
  60.3 55.0 %copy-start.6 = (s32[8]{0:T(128)S(1)}, s32[8]{0:T(128)}, u32[]{:S(2)}) copy-start(s32[8]{0:T(128)} %param.24) | copy-start | bytes 100
  190.1 75.3 %copy-start.1 = (bf16[6,512,512]{2,1,0:T(8,128)(2,1)S(1)}, bf16[6,512,512]{2,1,0:T(8,128)(2,1)}, u32[]{:S(2)}) copy-start(bf16[6,512,512]{2,1,0:T(8,128)(2,1)} %param.17) | copy-start | bytes 9437188
  257.4 7.2 %all-to-all-start.1 = ((f32[4,6,384]{2,0,1:T(4,128)}), f32[4,6,384]{2,0,1:T(4,128)S(1)}, u32[]{:S(2)}, u32[]{:S(2)}) async-start(f32[4,6,384]{2,0,1:T(4,128)} %copy.36), calls=%async_computation.2 | async-start | bytes 73728 | tf_op jit(solution)/shard_map/all_to_all | solution.py:123
Sparse Core Ops, SparseCore 0:
  13.1 41.2 all-gather.4
  201.2 54.6 reduce-scatter.1
where the time goes:
time: 273 us; the launch traced here: 272 us
  blocking collectives  134 us (49%)
  waiting for transfers between devices  58.6 us (21%)
  matrix products  36.3 us (13%)
  local copies, waits for them, and re-layouts  21.4 us (8%)
  between operations  14.3 us (5%)
  other arithmetic  4.47 us (2%)
  starting transfers between devices  3.3 us (1%)
    reduce_scatter x1, waiting for transfers between devices, on_device(): lax.psum_scatter(partial_out, 'seq', scatter_dimension=2, tiled=True)  54.9 us
    all_gather x2, blocking collectives, joined(): pieces = jax.tree.map(lambda part: lax.all_gather(part, axis), value)  42.1 us
    psum x1, blocking collectives, on_device(): lax.psum(jnp.dot(gained * scale_row[:, None], router_wide, precision=lax....  29.5 us
    psum x1, blocking collectives, on_device(): total_sq = lax.psum(squares, 'seq')  29.5 us
    all_gather x1, blocking collectives, on_device(): shard_rows = lax.all_gather(dispatched, 'seq', axis=2, tiled=True)  18.3 us
    dynamic_slice x15, local copies, waits for them, and re-layouts, joined(): lax.scan(lambda running, share: (join(running, share), None), head, tail)  13.4 us
    dot_general x1, matrix products, on_device(): jnp.einsum('erf,efd->erd', hidden_act, w_down, preferred_element_type=jnp...  10.9 us
    dot_general x1, matrix products, on_device(): jnp.einsum('ern,enf->erf', shard_rows, w_up, preferred_element_type=jnp.f...  9.94 us
  transfers between devices with their start and end apart: 3, of which 2 were waited for; matrix products, arithmetic and copies ran while one was open for 1% of the time, Pallas kernels for 0%

commit v1 on v0

v1 whole, which is shorter than its diff:
```python
import functools
import math

import jax
import jax.numpy as jnp
from jax import lax
from jax.experimental import pallas as pl
from jax.experimental.pallas import tpu as pltpu
from jax.sharding import PartitionSpec as P

MESH = pl.DeviceIdType.MESH
HEAD_DIM = 128
LANES = 128
masked_score = -1e30
norm_eps = 1e-05
F32 = jnp.float32
BF16 = jnp.bfloat16


def up(value, step):
    return -(-value // step) * step


def iota(shape, axis):
    return lax.broadcasted_iota(jnp.int32, shape, axis)


def div(value, by):
    return lax.div(value, jnp.full_like(value, by))


def rem(value, by):
    return lax.rem(value, jnp.full_like(value, by))


def dot(a, b):
    return jnp.dot(a, b, preferred_element_type=F32)


def attend_kernel(len_ref, q_ref, k_ref, v_ref, o_ref):
    b = pl.program_id(0)
    span = k_ref.shape[1]
    kvl, gp = q_ref.shape[1], q_ref.shape[2]
    first = lax.axis_index("seq") * span
    live = (iota((gp, span), 1) + first) < len_ref[b]
    lane = iota((gp, LANES), 1)
    for kv in range(kvl):
        cols = slice(kv * HEAD_DIM, (kv + 1) * HEAD_DIM)
        s = lax.dot_general(
            q_ref[0, kv], k_ref[0, :, cols], (((1,), (1,)), ((), ())), preferred_element_type=F32
        ) * (1.0 / math.sqrt(HEAD_DIM))
        s = jnp.where(live, s, masked_score)
        m = jnp.max(s, axis=1, keepdims=True).astype(BF16).astype(F32)
        w = jnp.where(live, jnp.exp(s - m), 0.0)
        l = jnp.sum(w, axis=1, keepdims=True)
        acc = dot(w.astype(BF16), v_ref[0, :, cols])
        l_hi = l.astype(BF16).astype(F32)
        stats = jnp.where(lane == 0, m, jnp.where(lane == 1, l_hi, jnp.where(lane == 2, l - l_hi, 0.0)))
        rows = slice(kv * gp, (kv + 1) * gp)
        o_ref[rows, :HEAD_DIM] = acc.astype(BF16)
        o_ref[rows, HEAD_DIM:] = stats.astype(BF16)


def ring_of(axis, count):
    me = lax.axis_index(axis)
    return me, [lax.rem(me + k, count) for k in range(count)], [lax.rem(me + count - k, count) for k in range(count)]


def merge_kernel(
    dims, x_ref, ids_ref, ow_hbm, hid_ref, gain_ref, rt_ref,
    xg_ref, st_ref, idv_ref, res_ref,
    ow, send1, recv1, buf2, buf3, buf4,
    ow_sem, ss1, rs1, ss2, rs2, ss3, rs3, ss4, rs4,
):
    n_seq, n_exp, seqs, toks, kvl, group, rv, rp = dims
    gp = up(group, 8)
    heads = kvl * group
    bp = buf3.shape[1]
    width = hid_ref.shape[1]
    me, to_seq, from_seq = ring_of("seq", n_seq)
    my_e, to_exp, from_exp = ring_of("exp", n_exp)

    barrier = pltpu.get_barrier_semaphore()
    for k in range(1, n_seq):
        pl.semaphore_signal(barrier, inc=1, device_id={"seq": to_seq[k]}, device_id_type=MESH)
    for k in range(1, n_exp):
        pl.semaphore_signal(barrier, inc=1, device_id={"exp": to_exp[k]}, device_id_type=MESH)
    ow_copy = pltpu.make_async_copy(ow_hbm, ow, ow_sem)
    ow_copy.start()

    src = iota((1, x_ref.shape[0]), 1)
    src_h = rem(src, kvl * gp)
    src_g = rem(src_h, gp)
    src_row = div(src, kvl * gp) * heads + div(src_h, gp) * group + src_g
    src_row = jnp.where(src_g < group, src_row, -1)
    slot = iota((n_seq * rp, 1), 0)
    slot_k = rem(slot, rp)
    slot_row = jnp.where(slot_k < rv, div(slot, rp) * rv + slot_k, -2)
    pack = (slot_row == src_row).astype(F32).astype(BF16)
    packed = dot(pack, x_ref[...]).astype(BF16)
    for p in range(n_seq):
        send1[p] = packed[p * rp:(p + 1) * rp]
    recv1[me] = send1[me]
    pl.semaphore_wait(barrier, n_seq + n_exp - 2)

    out1 = []
    for k in range(1, n_seq):
        c = pltpu.make_async_remote_copy(
            send1.at[to_seq[k]], recv1.at[me], ss1.at[k], rs1.at[k],
            device_id={"seq": to_seq[k]}, device_id_type=MESH)
        c.start()
        out1.append(c)
    for k in range(1, n_seq):
        pltpu.make_async_remote_copy(
            send1.at[to_seq[k]], recv1.at[from_seq[k]], ss1.at[k], rs1.at[k],
            device_id={"seq": to_seq[k]}, device_id_type=MESH).wait_recv()
    stats = [recv1[p][:, HEAD_DIM:].astype(F32) for p in range(n_seq)]
    peaks = [s[:, 0:1] for s in stats]
    top = functools.reduce(jnp.maximum, peaks)
    acc = jnp.zeros((rp, HEAD_DIM), F32)
    den = jnp.zeros((rp, 1), F32)
    for p in range(n_seq):
        f = jnp.exp(peaks[p] - top)
        den = den + (stats[p][:, 1:2] + stats[p][:, 2:3]) * f
        acc = acc + recv1[p][:, :HEAD_DIM].astype(F32) * f
    att = jnp.where(den > 0.0, acc / jnp.where(den > 0.0, den, 1.0), 0.0)
    buf2[me] = att.astype(BF16)

    def gather(buf, sends, recvs, axis, mine, to, frm):
        started = []
        for k in range(1, len(to)):
            c = pltpu.make_async_remote_copy(
                buf.at[mine], buf.at[mine], sends.at[k], recvs.at[k],
                device_id={axis: to[k]}, device_id_type=MESH)
            c.start()
            started.append(c)
        for k in range(1, len(to)):
            pltpu.make_async_remote_copy(
                buf.at[mine], buf.at[frm[k]], sends.at[k], recvs.at[k],
                device_id={axis: to[k]}, device_id_type=MESH).wait_recv()
        return started

    out2 = gather(buf2, ss2, rs2, "seq", me, to_seq, from_seq)
    row = iota((heads * bp, 1), 0)
    row_b = rem(row, bp)
    want = jnp.where(row_b < seqs, row_b * heads + div(row, bp), -3)
    slot = iota((1, n_seq * rp), 1)
    slot_k = rem(slot, rp)
    have = jnp.where(slot_k < rv, div(slot, rp) * rv + slot_k, -2)
    unpack = (want == have).astype(F32).astype(BF16)
    rows = dot(unpack, jnp.concatenate([buf2[p] for p in range(n_seq)], axis=0))
    att_all = jnp.concatenate([rows[h * bp:(h + 1) * bp] for h in range(heads)], axis=1).astype(BF16)
    ow_copy.wait()
    part = dot(att_all, ow[...])
    hid = hid_ref[...].astype(F32)
    rowc = iota((bp, width), 0)
    rowl = iota((bp, LANES), 0)
    lane = iota((bp, LANES), 1)
    idv = jnp.zeros((bp, LANES), F32)
    for t in range(toks):
        at = my_e * toks + t
        part = part + jnp.where(rowc == at, hid[t:t + 1, :], 0.0)
        for k in range(2):
            idv = idv + jnp.where((rowl == at) & (lane == k), ids_ref[t, k].astype(F32), 0.0)
    buf3[my_e, :, :width] = part
    buf3[my_e, :, width:] = idv
    out3 = gather(buf3, ss3, rs3, "exp", my_e, to_exp, from_exp)
    total = functools.reduce(lambda a, b: a + b, [buf3[e] for e in range(n_exp)])
    residual = total[:, :width]
    idv_ref[...] = total[:, width:].astype(jnp.int32)
    for t in range(toks):
        mine = jnp.sum(jnp.where(rowc == my_e * toks + t, residual, 0.0), axis=0, keepdims=True)
        res_ref[t:t + 1, :] = mine
    gained = residual * gain_ref[...]
    logit = jnp.dot(gained, rt_ref[...].astype(F32), precision=lax.Precision.HIGHEST, preferred_element_type=F32)
    square = jnp.sum(residual * residual, axis=1, keepdims=True)
    st = jnp.where(lane == 15, square, logit)
    hi = st.astype(BF16).astype(F32)
    buf4[me, :, :width] = gained.astype(BF16)
    buf4[me, :, width:] = (hi + pltpu.roll(st - hi, 16, 1)).astype(BF16)
    out4 = gather(buf4, ss4, rs4, "seq", me, to_seq, from_seq)
    tot = jnp.zeros((bp, LANES), F32)
    for p in range(n_seq):
        xg_ref[:, p * width:(p + 1) * width] = buf4[p, :, :width]
        tot = tot + buf4[p, :, width:].astype(F32)
    st_ref[...] = tot + pltpu.roll(tot, LANES - 16, 1)
    for c in out1 + out2 + out3 + out4:
        c.wait_send()


def expert_kernel(
    dims, ids_ref, cap_ref, xg_ref, st_ref, idv_ref, wg_hbm, wu_hbm, wd_hbm,
    o_ref, gate, upb, down, y, coef, order, sems,
):
    n_seq, n_exp, seqs, toks, n_experts, chunk = dims
    local = wg_hbm.shape[0]
    bp, model = xg_ref.shape
    width = model // n_seq
    slots = gate.shape[0]
    chunks = wg_hbm.shape[2] // chunk
    first = lax.axis_index("exp") * local

    count = jnp.int32(0)
    for e in range(local):
        named = jnp.int32(0)
        for b in range(seqs):
            for k in range(2):
                named = named | (ids_ref[b, k] == first + e).astype(jnp.int32)

        @pl.when(named > 0)
        def _():
            order[count] = e

        count = count + named
    steps = count * chunks

    def copies(i):
        s = lax.rem(i, slots)
        e = order[lax.div(i, chunks)]
        at = pl.multiple_of(lax.rem(i, chunks) * chunk, chunk)
        return (
            pltpu.make_async_copy(wg_hbm.at[e, :, pl.ds(at, chunk)], gate.at[s], sems.at[s, 0]),
            pltpu.make_async_copy(wu_hbm.at[e, :, pl.ds(at, chunk)], upb.at[s], sems.at[s, 1]),
            pltpu.make_async_copy(wd_hbm.at[e, pl.ds(at, chunk), :], down.at[s], sems.at[s, 2]),
        )

    for i in range(slots - 1):
        @pl.when(i < steps)
        def _():
            for c in copies(jnp.int32(i)):
                c.start()

    st = st_ref[...]
    lane = iota((bp, LANES), 1)
    rowc = iota((bp, 1), 0)
    scale = lax.rsqrt(st[:, 15:16] / model + norm_eps)
    logits = jnp.where(lane < n_experts, st, 0.0) * scale
    ids = [idv_ref[:, k:k + 1] for k in range(2)]
    chosen = [jnp.sum(jnp.where(lane == ids[k], logits, 0.0), axis=1, keepdims=True) for k in range(2)]
    weight = []
    for k in range(2):
        rank = jnp.zeros((bp, 1), jnp.int32)
        for b in range(seqs):
            end = (b // toks + 1) * toks
            later = (rowc > b) & (rowc < end)
            for j in range(2):
                rank = rank + jnp.where(later & (ids[k] == ids_ref[b, j]), 1, 0)
        limit = jnp.zeros((bp, 1), jnp.int32)
        for e in range(n_experts):
            limit = limit + jnp.where(ids[k] == e, cap_ref[e], 0)
        keep = (rank < limit) & (rowc < seqs)
        weight.append(jnp.where(keep, jax.nn.sigmoid(chosen[k] - chosen[1 - k]), 0.0))
    coef[0] = jnp.broadcast_to(weight[0], (bp, LANES))
    coef[1] = jnp.broadcast_to(weight[1], (bp, LANES))
    y[...] = jnp.zeros_like(y)

    def step(i, carry):
        for c in copies(i):
            c.wait()

        @pl.when(i + slots - 1 < steps)
        def _():
            for c in copies(i + slots - 1):
                c.start()

        s = lax.rem(i, slots)
        e = order[lax.div(i, chunks)] + first
        x = xg_ref[...]
        g = dot(x, gate[s]) * scale
        u = dot(x, upb[s]) * scale
        h = (jax.nn.silu(g) * u).astype(BF16)
        c = jnp.where(ids[0] == e, coef[0][:, :1], 0.0) + jnp.where(ids[1] == e, coef[1][:, :1], 0.0)
        y[...] += dot(h, down[s]) * c
        return carry

    lax.fori_loop(0, steps, step, jnp.int32(0))
    for e in range(n_exp):
        rows = y[e * toks:(e + 1) * toks, :].astype(BF16)
        for s in range(n_seq):
            o_ref[e * n_seq + s] = rows[:, s * width:(s + 1) * width]


def scatter_kernel(dims, y_ref, res_ref, o_ref, recv, ss, rs):
    n_seq, n_exp = dims
    n = n_seq * n_exp
    me = lax.axis_index("exp") * n_seq + lax.axis_index("seq")
    to = [lax.rem(me + k, n) for k in range(n)]
    frm = [lax.rem(me + n - k, n) for k in range(n)]

    def where(p):
        return {"seq": lax.rem(p, n_seq), "exp": lax.div(p, n_seq)}

    barrier = pltpu.get_barrier_semaphore()
    for k in range(1, n):
        pl.semaphore_signal(barrier, inc=1, device_id=where(to[k]), device_id_type=MESH)
    recv[me] = y_ref[me]
    pl.semaphore_wait(barrier, n - 1)
    started = []
    for k in range(1, n):
        c = pltpu.make_async_remote_copy(
            y_ref.at[to[k]], recv.at[me], ss.at[k], rs.at[k],
            device_id=where(to[k]), device_id_type=MESH)
        c.start()
        started.append(c)
    for k in range(1, n):
        pltpu.make_async_remote_copy(
            y_ref.at[to[k]], recv.at[frm[k]], ss.at[k], rs.at[k],
            device_id=where(to[k]), device_id_type=MESH).wait_recv()
    total = res_ref[...]
    for p in range(n):
        total = total + recv[p].astype(F32)
    o_ref[...] = total.astype(BF16)
    for c in started:
        c.wait_send()


def on_device(
    n_seq, n_exp, hidden_in, queries, key_cache, value_cache, lengths, out_weight, norm_gain,
    router, expert_ids, capacity, w_gate, w_up, w_down,
):
    seqs = queries.shape[0]
    toks, width = hidden_in.shape
    span = key_cache.shape[1]
    kvl = key_cache.shape[2] // HEAD_DIM
    heads = queries.shape[1] // HEAD_DIM
    group = heads // kvl
    gp = up(group, 8)
    bp = up(seqs, 8)
    n_experts = router.shape[1]
    model = width * n_seq
    rv = -(-seqs * heads // n_seq)
    rp = up(rv, 16)
    vmem = pl.BlockSpec(memory_space=pltpu.VMEM)
    smem = pl.BlockSpec(memory_space=pltpu.SMEM)
    hbm = pl.BlockSpec(memory_space=pltpu.HBM)
    q = jnp.pad(queries.reshape(seqs, kvl, group, HEAD_DIM), ((0, 0), (0, 0), (0, gp - group), (0, 0)))
    partial = pl.pallas_call(
        attend_kernel,
        grid=(seqs,),
        in_specs=[
            smem,
            pl.BlockSpec((1, kvl, gp, HEAD_DIM), lambda b: (b, 0, 0, 0)),
            pl.BlockSpec((1, span, kvl * HEAD_DIM), lambda b: (b, 0, 0)),
            pl.BlockSpec((1, span, kvl * HEAD_DIM), lambda b: (b, 0, 0)),
        ],
        out_specs=pl.BlockSpec((kvl * gp, 2 * HEAD_DIM), lambda b: (b, 0)),
        out_shape=jax.ShapeDtypeStruct((seqs * kvl * gp, 2 * HEAD_DIM), BF16),
        name="attend",
    )(lengths, q, key_cache, value_cache)

    dma = pltpu.SemaphoreType.DMA
    rt = jnp.pad(router, ((0, 0), (0, LANES - n_experts)))
    xg, st, idv, res = pl.pallas_call(
        functools.partial(merge_kernel, (n_seq, n_exp, seqs, toks, kvl, group, rv, rp)),
        in_specs=[vmem, smem, hbm, vmem, vmem, vmem],
        out_specs=[vmem] * 4,
        out_shape=[
            jax.ShapeDtypeStruct((bp, model), BF16),
            jax.ShapeDtypeStruct((bp, LANES), F32),
            jax.ShapeDtypeStruct((bp, LANES), jnp.int32),
            jax.ShapeDtypeStruct((toks, width), F32),
        ],
        scratch_shapes=[
            pltpu.VMEM(out_weight.shape, BF16),
            pltpu.VMEM((n_seq, rp, 2 * HEAD_DIM), BF16),
            pltpu.VMEM((n_seq, rp, 2 * HEAD_DIM), BF16),
            pltpu.VMEM((n_seq, rp, HEAD_DIM), BF16),
            pltpu.VMEM((n_exp, bp, width + LANES), F32),
            pltpu.VMEM((n_seq, bp, width + LANES), BF16),
            dma,
            dma((n_seq,)), dma((n_seq,)), dma((n_seq,)), dma((n_seq,)),
            dma((n_exp,)), dma((n_exp,)), dma((n_seq,)), dma((n_seq,)),
        ],
        compiler_params=pltpu.CompilerParams(collective_id=0, has_side_effects=True),
        name="merge",
    )(partial, expert_ids, out_weight, hidden_in, norm_gain.reshape(1, width), rt)

    chunk = min(256, w_gate.shape[2])
    slots = 3
    y = pl.pallas_call(
        functools.partial(expert_kernel, (n_seq, n_exp, seqs, toks, n_experts, chunk)),
        in_specs=[smem, smem, vmem, vmem, vmem, hbm, hbm, hbm],
        out_specs=vmem,
        out_shape=jax.ShapeDtypeStruct((n_exp * n_seq, toks, width), BF16),
        scratch_shapes=[
            pltpu.VMEM((slots, model, chunk), BF16),
            pltpu.VMEM((slots, model, chunk), BF16),
            pltpu.VMEM((slots, chunk, model), BF16),
            pltpu.VMEM((bp, model), F32),
            pltpu.VMEM((2, bp, LANES), F32),
            pltpu.SMEM((w_gate.shape[0],), jnp.int32),
            dma((slots, 3)),
        ],
        compiler_params=pltpu.CompilerParams(vmem_limit_bytes=48 * 1024 * 1024),
        name="experts",
    )(idv, capacity, xg, st, idv, w_gate, w_up, w_down)

    return pl.pallas_call(
        functools.partial(scatter_kernel, (n_seq, n_exp)),
        in_specs=[vmem, vmem],
        out_specs=vmem,
        out_shape=jax.ShapeDtypeStruct((toks, width), BF16),
        scratch_shapes=[
            pltpu.VMEM((n_exp * n_seq, toks, width), BF16),
            dma((n_exp * n_seq,)), dma((n_exp * n_seq,)),
        ],
        compiler_params=pltpu.CompilerParams(collective_id=1, has_side_effects=True),
        name="scatter",
    )(y, res)


def solution(mesh):
    in_specs = (
        P("exp", "seq"),
        P(None, "exp"),
        P(None, "seq", "exp"),
        P(None, "seq", "exp"),
        P(),
        P("exp", "seq"),
        P("seq"),
        P("seq", None),
        P("exp", None),
        P(),
        P("exp", None, "seq"),
        P("exp", None, "seq"),
        P("exp", "seq", None),
    )
    return jax.shard_map(
        functools.partial(on_device, mesh.shape["seq"], mesh.shape["exp"]),
        mesh=mesh, in_specs=in_specs, out_specs=P("exp", "seq"), check_vma=False,
    )
```

time: 273 us -> 74.8 us (0.27)
  blocking collectives: 134 us -> 0 us
  Pallas kernels: 0 us -> 63.4 us
  waiting for transfers between devices: 58.6 us -> 0 us
  matrix products: 36.3 us -> 0 us
  between operations: 14.3 us -> 0.05 us
  local copies, waits for them, and re-layouts: 21.4 us -> 10.4 us
  other arithmetic: 4.47 us -> 0 us
  starting transfers between devices: 3.3 us -> 0 us
    pallas_call x0 -> x4, Pallas kernels: none -> 63.4 us  [the longest x1 25.5 us: on_device(): pl.pallas_call(functools.partial(merge_kernel, (n_seq, n_exp, seqs, toks,...]
    all_gather x3 -> x0, blocking collectives: 60.3 us -> none  [the longest x2 42.1 us: joined(): pieces = jax.tree.map(lambda part: lax.all_gather(part, axis), value)]
    psum x2 -> x0, blocking collectives: 59 us -> none  [the longest x1 29.5 us: on_device(): lax.psum(jnp.dot(gained * scale_row[:, None], router_wide, precision=lax....]
    reduce_scatter x1 -> x0, waiting for transfers between devices: 54.9 us -> none  [on_device(): lax.psum_scatter(partial_out, 'seq', scatter_dimension=2, tiled=True)]
    dot_general x12 -> x0, matrix products: 36.3 us -> none  [the longest x1 10.9 us: on_device(): jnp.einsum('erf,efd->erd', hidden_act, w_down, preferred_element_type=jnp...]
    dynamic_slice x15 -> x0, local copies, waits for them, and re-layouts: 13.4 us -> none  [joined(): lax.scan(lambda running, share: (join(running, share), None), head, tail)]
    unnamed x1 -> x0, blocking collectives: 8.06 us -> none
    all_to_all x1 -> x0, blocking collectives: 6.25 us -> none  [on_device(): lax.all_to_all(buffer, 'exp', split_axis=0, concat_axis=1, tiled=True)]
  transfers between devices with their start and end apart: 3 -> 0, of which waited for: 2 -> 0; matrix products, arithmetic and copies ran while one was open for 1% -> 0% of each run, Pallas kernels for 0% -> 0%
where the time goes in v1:
time: 74.8 us; the launch traced here: 73.8 us
  Pallas kernels  63.4 us (85%)
  local copies, waits for them, and re-layouts  10.4 us (14%)
    pallas_call x1, Pallas kernels, on_device(): pl.pallas_call(functools.partial(merge_kernel, (n_seq, n_exp, seqs, toks,...  25.5 us
    pallas_call x1, Pallas kernels, on_device(): pl.pallas_call(functools.partial(scatter_kernel, (n_seq, n_exp)), in_spec...  15.1 us
    pallas_call x1, Pallas kernels, on_device(): pl.pallas_call(functools.partial(expert_kernel, (n_seq, n_exp, seqs, toks...  14.2 us
    pallas_call x1, Pallas kernels, on_device(): pl.pallas_call(attend_kernel, grid=(seqs,), in_specs=[smem, pl.BlockSpec(...  8.66 us
    unnamed x13, local copies, waits for them, and re-layouts  6.95 us

profile of v1, /device:TPU:0, one launch (start us, length us, event | category | flops | bytes accessed | tf_op | source)
XLA Modules:
  0.0 73.8 jit_solution(14269819786556644987)
XLA Ops:
  0.0 1.3 %reshape.7.gain_ref = f32[1,384]{1,0:T(1,128)} reshape(f32[384]{0:T(512)} %param.19) | data formatting | bytes 3072 | tf_op jit(solution)/shard_map/reshape | solution.py:376
  1.3 1.3 %copy.17.ids_ref = s32[3,2]{1,0:T(4,128)} copy(s32[3,2]{0,1:T(2,128)} %param.21) | data formatting | bytes 48 | tf_op args[8]
  2.6 0.9 %reshape.6 = bf16[6,4,6,128]{3,2,1,0:T(8,128)(2,1)S(1)} reshape(bf16[6,3072]{1,0:T(8,128)(2,1)} %param.14) | data formatting | bytes 73728 | tf_op jit(solution)/shard_map/reshape | solution.py:336
  3.5 0.6 pad.8.q_ref
  4.1 8.7 %attend.1.x_ref = bf16[192,256]{1,0:T(8,128)(2,1)} custom-call(s32[6]{0:T(128)} %len_ref.1, bf16[6,4,8,128]{3,2,1,0:T(8,128)(2,1)} %pad.8.q_ref, bf16[6,512,512]{2,1,0:T(8,128)(2,1)} %k_ref.1, bf16[6,512,512]{2,1,0:T(8,128)(2,1)} %v_ref.1), custom_call_target="tpu_custom_call" | custom-call | tf_op jit(solution)/shard_map/attend/pallas_call | solution.py:337
  12.8 0.8 %copy.16 = bf16[384,8]{1,0:T(8,128)(2,1)S(1)} copy(bf16[384,8]{0,1:T(8,128)(2,1)} %param.20) | data formatting | bytes 12288 | tf_op args[7]
  13.6 0.7 pad.9.rt_ref
  14.3 25.5 %merge.1 = (bf16[8,6144]{1,0:T(8,128)(2,1)}, f32[8,128]{1,0:T(8,128)}, s32[8,128]{1,0:T(8,128)}, f32[3,384]{1,0:T(4,128)}) custom-call(bf16[192,256]{1,0:T(8,128)(2,1)} %attend.1.x_ref, s32[3,2]{1,0:T(4,128)} %copy.17.ids_ref, bf16[3072,384]{1,0:T(8,128)(2,1)} %ow_hbm.1, bf16[3,384]{1,0:T(4,128)(2,1)} %hid_ref.1, f32[1,384]{1,0:T(1,128)} %reshape.7.gain_ref, ...), custom_call_target="tpu_custom_call" | custom-call | tf_op jit(solution)/shard_map/merge/pallas_call | solution.py:353
  39.7 0.0 copy-start.1
  39.8 0.9 %copy-done.1 = bf16[8,6144]{1,0:T(8,128)(2,1)S(1)} copy-done((bf16[8,6144]{1,0:T(8,128)(2,1)S(1)}, bf16[8,6144]{1,0:T(8,128)(2,1)}, u32[]{:S(2)}) %copy-start.1) | copy-done | bytes 98328
  40.6 0.0 copy-start.2
  40.6 0.7 copy-done.2
  41.3 0.0 copy-start.3
  41.3 0.7 copy-done.3
  42.0 0.0 copy-start.4
  42.0 0.7 copy-done.4
  42.6 14.2 %experts.1.y_ref = bf16[32,3,384]{2,1,0:T(4,128)(2,1)S(1)} custom-call(s32[8,128]{1,0:T(8,128)S(1)} %copy-done.2, s32[8]{0:T(128)S(1)} %copy-done.4, bf16[8,6144]{1,0:T(8,128)(2,1)S(1)} %copy-done.1, f32[8,128]{1,0:T(8,128)S(1)} %copy-done.3, s32[8,128]{1,0:T(8,128)S(1)} %copy-done.2, bf16[4,6144,512]{2,1,0:T(8,128)(2,1)} %wg_hbm.1, ...), custom_call_target="tpu_custom_call" | custom-call | tf_op jit(solution)/shard_map/experts/pallas_call | solution.py:380
  56.9 0.0 copy-start
  56.9 0.6 copy-done
  57.5 15.1 %scatter.1 = bf16[3,384]{1,0:T(4,128)(2,1)} custom-call(bf16[32,3,384]{2,1,0:T(4,128)(2,1)} %copy-done, f32[3,384]{1,0:T(4,128)} %get-tuple-element.12.res_ref), custom_call_target="tpu_custom_call" | custom-call | tf_op jit(solution)/shard_map/scatter/pallas_call | solution.py:398
  72.6 1.2 %copy.19 = bf16[3,384]{1,0:T(4,128)(2,1)} copy(bf16[3,384]{1,0:T(4,128)(2,1)} %scatter.1) | data formatting | bytes 4608
Async XLA Ops:
  39.7 0.9 %copy-start.1 = (bf16[8,6144]{1,0:T(8,128)(2,1)S(1)}, bf16[8,6144]{1,0:T(8,128)(2,1)}, u32[]{:S(2)}) copy-start(bf16[8,6144]{1,0:T(8,128)(2,1)} %get-tuple-element.10.xg_ref) | copy-start | bytes 294916
  40.6 0.7 copy-start.2
  41.3 0.7 copy-start.3
  42.0 0.7 copy-start.4
  56.9 0.6 copy-start
